TPU v7x, 8 devices: a whole 2x2x1 slice. The times are simulated.
8 devices in a mesh: dp: 2 (over y, z), sp: 4 (over x, core).
Axes of the slice: x: 2, y: 2, z: 1, core: 2. Of those that a mesh axis runs over, the one named last changes fastest.
Arguments:
- q: bfloat16 [64, 96, 128], P('dp'), parts along dimension 0
- k: bfloat16 [64, 8192, 8, 128], P('dp', 'sp'), parts along dimension 0
- v: bfloat16 [64, 8192, 8, 128], P('dp', 'sp'), parts along dimension 0
Outputs:
- q: bfloat16 [64, 96, 128], P('dp'), parts along dimension 0
There are 2 independent parts. A program takes and returns all parts, laid end to end along the dimension named above; each array names one.
All inputs are finite; a program needn't handle non-finite values.
Results may differ from a plain program's by a relative error of at most 0.012.
Values are sent between devices in bfloat16 or wider.
A program may use at most 2 GiB of HBM per device.

v0:
```python
import jax
import jax.numpy as jnp
from jax import lax
from jax.sharding import PartitionSpec as P


def einsum(form, a, b):
    return jnp.einsum(form, a.astype(jnp.float32), b.astype(jnp.float32))


def part_of(q, k, v):
    grouped = q.reshape(q.shape[0], k.shape[2], -1, q.shape[2])
    scores = einsum("bgsd,bugd->bgsu", grouped, k) * q.shape[2] ** -0.5
    high = jnp.max(scores, -1, keepdims=True)
    weights = jnp.exp(scores - high)
    seen = einsum("bgsu,bugd->bgsd", weights.astype(jnp.bfloat16), v)
    return jnp.concatenate([seen, jnp.sum(weights, -1, keepdims=True), high], -1)


def together(parts):
    seen, total, high = parts[..., :-2], parts[..., -2:-1], parts[..., -1:]
    scale = jnp.exp(high - jnp.max(high, 0))
    return (jnp.sum(seen * scale, 0) / jnp.sum(total * scale, 0)).astype(jnp.bfloat16)


def solution(mesh):
    def step(q, k, v):
        return together(lax.all_gather(part_of(q, k, v), "sp")).reshape(q.shape)

    return jax.shard_map(
        step,
        mesh=mesh,
        in_specs=(P("dp", None, None), P("dp", "sp", None, None), P("dp", "sp", None, None)),
        out_specs=P("dp", None, None),
        check_vma=False,
    )
```

profile of v0, /device:TPU:0, one launch (start us, length us, event | category | flops | bytes accessed | tf_op | source)
XLA Modules:
  0.0 277.7 jit_solution(15026884133890713835)
XLA Ops:
  6.5 0.0 all-gather.3.cloned.1.call-start
  6.5 1.4 copy.46
  8.0 68.3 %multiply_reduce_fusion = (f32[32,8,12]{2,1,0:T(8,128)S(1)}, f32[32,8,12,2048]{3,2,1,0:T(8,128)}) fusion(bf16[32,2048,8,128]{3,2,1,0:T(8,128)(2,1)} %param.4, bf16[32,8,12,128]{3,0,2,1:T(8,128)(2,1)S(1)} %bitcast.14), kind=kOutput, calls=%fused_computation.5 | convolution fusion | flops 1623192576 | bytes 160182272 | tf_op jit(solution)/shard_map/bgsd,bugd->bgsu/dot_general | solution.py:8
  76.3 14.2 %fusion.4 = f32[32,8,12]{2,1,0:T(8,128)S(1)} fusion(f32[32,8,12,2048]{3,2,1,0:T(8,128)} %get-tuple-element.11, f32[32,8,12]{2,1,0:T(8,128)S(1)} %get-tuple-element.10), kind=kLoop, calls=%fused_computation.6 | loop fusion | flops 18871296 | bytes 25190400 | tf_op jit(solution)/shard_map/reduce_sum | solution.py:17
  90.5 55.0 %fusion = f32[32,8,12,128]{3,2,1,0:T(8,128)} fusion(bf16[32,2048,8,128]{3,2,1,0:T(8,128)(2,1)} %param.5, f32[32,8,12,2048]{3,2,1,0:T(8,128)} %get-tuple-element.11, f32[32,8,12]{2,1,0:T(8,128)S(1)} %get-tuple-element.10), kind=kOutput, calls=%fused_computation | convolution fusion | flops 1629487104 | bytes 160968704 | tf_op jit(solution)/shard_map/bgsu,bugd->bgsd/dot_general | solution.py:8
  145.6 1.7 copy.52
  147.2 3.0 %copy.53 = f32[32,8,12,1]{3,2,1,0:T(8,128)} copy(f32[32,8,12,1]{2,1,0,3:T(8,128)S(1)} %bitcast.15) | data formatting | bytes 24576 | tf_op jit(solution)/shard_map/broadcast_in_dim | solution.py:14
  150.3 3.0 %pad_maximum_fusion = f32[32,8,12,130]{3,2,1,0:T(8,128)S(1)} fusion(f32[32,8,12,1]{3,2,1,0:T(8,128)} %copy.53, f32[32,8,12,1]{3,2,1,0:T(8,128)S(1)} %copy.52, f32[32,8,12,128]{3,2,1,0:T(8,128)} %fusion), kind=kLoop, calls=%fused_computation.12 | loop fusion | flops 798720 | bytes 3194880 | tf_op jit(solution)/shard_map/concatenate | solution.py:17
  153.3 4.5 %copy.54 = f32[32,8,12,130]{3,1,2,0:T(8,128)} copy(f32[32,8,12,130]{3,2,1,0:T(8,128)S(1)} %pad_maximum_fusion) | data formatting | bytes 3194880 | tf_op jit(solution)/shard_map/concatenate | solution.py:17
  157.8 0.0 all-gather.3.cloned.1.call-update
  157.9 82.9 %all-gather.3.cloned.1.call-done = f32[128,8,12,130]{3,1,2,0:T(8,128)} async-done(((f32[32,8,12,130]{3,1,2,0:T(8,128)}), f32[128,8,12,130]{3,1,2,0:T(8,128)}) %all-gather.3.cloned.1.call-update) | async-done | bytes 6389776 | tf_op jit(solution)/shard_map/all_gather | solution.py:28
  240.8 11.6 %fusion.14 = (f32[4,32,8,12,1]{4,2,3,1,0:T(8,128)}, f32[32,8,12]{1,2,0:T(8,128)S(1)}, f32[4,32,8,12,1]{4,2,3,1,0:T(8,128)}) fusion(f32[4,32,8,12,130]{4,2,3,1,0:T(8,128)} %bitcast.12), kind=kLoop, calls=%fused_computation.21 | loop fusion | flops 9216 | bytes 208896 | tf_op jit(solution)/shard_map/slice | solution.py:21
  252.4 5.2 %copy.68 = f32[4,32,8,12,1]{1,2,4,3,0:T(8,128)S(1)} copy(f32[4,32,8,12,1]{4,2,3,1,0:T(8,128)} %get-tuple-element.5) | data formatting | bytes 98304
  257.6 0.1 copy.70
  257.8 5.2 %copy.67 = f32[4,32,8,12,1]{1,2,4,3,0:T(8,128)S(1)} copy(f32[4,32,8,12,1]{4,2,3,1,0:T(8,128)} %get-tuple-element.7) | data formatting | bytes 98304
  263.1 0.5 copy.56
  263.6 4.6 %fusion.9 = f32[32,8,12,128]{3,1,2,0:T(8,128)S(1)} fusion(f32[4,32,8,12,130]{4,2,3,1,0:T(8,128)} %bitcast.13, f32[4,32,8,12]{2,3,1,0:T(8,128)S(1)} %copy.56), kind=kLoop, calls=%fused_computation.11 | loop fusion | flops 2752512 | bytes 7913472 | tf_op jit(solution)/shard_map/reduce_sum | solution.py:23
  268.2 0.9 copy.58
  269.1 0.5 fusion.10
  269.6 1.2 copy.61
  (3 shorter events, 0.1 us)
Async XLA Ops:
  6.5 234.3 %all-gather.3.cloned.1.call-start = ((), (), s32[]{:S(2)}) async-start(), calls=%async_computation | async-start | bytes 15728640 | tf_op jit(solution)/shard_map/all_gather | solution.py:28
Sparse Core Ops, SparseCore 0:
  158.0 82.7 all-gather.2
where the time goes:
time: 278 us
  matrix products  123 us (44%)
  waiting for transfers between devices  83 us (30%)
  other arithmetic  34.1 us (12%)
  local copies, waits for them, and re-layouts  23.8 us (9%)
  between operations  13.5 us (5%)
    dot_general x2, matrix products, einsum(): return jnp.einsum(form, a.astype(jnp.float32), b.astype(jnp.float32))  123 us
    all_gather x1, waiting for transfers between devices, step(): return together(lax.all_gather(part_of(q, k, v), 'sp')).reshape(q.shape)  82.9 us
    reduce_sum x1, other arithmetic, part_of(): jnp.sum(weights, -1, keepdims=True)  14.2 us
    unnamed x4, local copies, waits for them, and re-layouts  12 us
    slice x1, other arithmetic, together(): seen, total, high = (parts[..., :-2], parts[..., -2:-1], parts[..., -1:])  11.6 us
  transfers between devices with their start and end apart: 1, of which 1 were waited for; matrix products, arithmetic and copies ran while one was open for 0% of the time, Pallas kernels for 0%

commit v1 on v0

v1 whole, which is shorter than its diff:
```python
import jax
import jax.numpy as jnp
from jax import lax
from jax.experimental import pallas as pl
from jax.experimental.pallas import tpu as pltpu
from jax.sharding import PartitionSpec as P

NBUF = 3


def local_attention(q, k, v):
    seqs, heads, head = q.shape
    length, kv_heads = k.shape[1:3]
    share = heads // kv_heads
    half = heads // 2
    pairs = kv_heads // 2
    rows = 2 * length
    scale = head**-0.5 * 1.4426950408889634
    k = k.reshape(seqs, length, pairs, 2, head)
    v = v.reshape(seqs, length, pairs, 2, head)

    def kern(q_ref, k_hbm, v_hbm, o_ref, st_ref, kb, vb, sb, sem):
        def copies(b, slot, a):
            src, dst = ((k_hbm, kb), (v_hbm, vb))[a]
            return [pltpu.make_async_copy(src.at[b, :, i], dst.at[slot, i], sem.at[slot, a, i]) for i in range(pairs)]

        def both(ref, slot, j, lo):
            part = [ref.at[slot, 2 * j + i].reshape(rows, head)[pl.ds(lo, 256), :] for i in range(2)]
            return jnp.concatenate(part, 1)

        for s in range(NBUF - 1):
            for a in range(2):
                for c in copies(s, s, a):
                    c.start()
        row = lax.broadcasted_iota(jnp.int32, (half, 256), 0)
        lane = lax.broadcasted_iota(jnp.int32, (half, 256), 1)
        valid = lax.rem(lax.div(row, share), 2) == lax.rem(lane, 2)
        first = lax.broadcasted_iota(jnp.int32, (half, head), 0) < half // 2

        @pl.loop(0, seqs)
        def _(b):
            slot = lax.rem(b, NBUF)
            nx = b + NBUF - 1

            @pl.when(nx < seqs)
            def _():
                for a in range(2):
                    for c in copies(nx, lax.rem(nx, NBUF), a):
                        c.start()

            for c in copies(b, slot, 0):
                c.wait()
            ms = []
            for j in range(2):
                qj = q_ref[b, pl.ds(half * j, half), :]
                z = jnp.zeros_like(qj)
                q2 = jnp.concatenate([jnp.where(first, qj, z), jnp.where(first, z, qj)], 1)
                mx = jnp.full((half, head), -jnp.inf, jnp.float32)
                for n in range(rows // 256):
                    s = lax.dot_general(q2, both(kb, slot, j, n * 256), (((1,), (1,)), ((), ())), preferred_element_type=jnp.float32)
                    s = jnp.where(valid, s, -jnp.inf)
                    sb[j, :, pl.ds(n * 256, 256)] = s
                    mx = jnp.maximum(mx, jnp.maximum(s[:, :128], s[:, 128:]))
                ms.append(jnp.max(mx, 1, keepdims=True))
            for c in copies(b, slot, 1):
                c.wait()
            for j in range(2):
                l = jnp.zeros((half, head), jnp.float32)
                o = jnp.zeros((half, 256), jnp.float32)
                for n in range(rows // 256):
                    p = jnp.exp2((sb[j, :, pl.ds(n * 256, 256)] - ms[j]) * scale)
                    l = l + p[:, :128] + p[:, 128:]
                    o = o + jnp.dot(p.astype(jnp.bfloat16), both(vb, slot, j, n * 256), preferred_element_type=jnp.float32)
                l = jnp.sum(l, 1, keepdims=True)
                o_ref[b, pl.ds(half * j, half), :] = jnp.where(first, o[:, :head], o[:, head:]).astype(jnp.bfloat16)
                ln = lax.broadcasted_iota(jnp.int32, (half, head), 1)
                st_ref[b, pl.ds(half * j, half), :] = jnp.where(ln == 0, l, ms[j])

    buf = pltpu.VMEM((NBUF, pairs, length, 2, head), jnp.bfloat16)
    o, st = pl.pallas_call(
        kern,
        out_shape=[jax.ShapeDtypeStruct((seqs, heads, head), jnp.bfloat16), jax.ShapeDtypeStruct((seqs, heads, head), jnp.float32)],
        in_specs=[pl.BlockSpec(memory_space=pltpu.VMEM)] + [pl.BlockSpec(memory_space=pl.ANY)] * 2,
        scratch_shapes=[buf, buf, pltpu.VMEM((2, half, rows), jnp.float32), pltpu.SemaphoreType.DMA((NBUF, 2, pairs))],
        compiler_params=pltpu.CompilerParams(vmem_limit_bytes=60 << 20),
    )(q, k, v)
    return o, st[..., 0], st[..., 1]


def solution(mesh):
    def step(q, k, v):
        o, l, m = local_attention(q, k, v)
        o = lax.all_gather(o, "sp").astype(jnp.float32)
        st = lax.all_gather(jnp.stack([l, m]), "sp")
        l, m = st[:, 0], st[:, 1]
        w = jnp.exp2((m - jnp.max(m, 0)) * (q.shape[2] ** -0.5 * 1.4426950408889634))
        return (jnp.sum(o * w[..., None], 0) / jnp.sum(l * w, 0)[..., None]).astype(jnp.bfloat16)

    return jax.shard_map(
        step,
        mesh=mesh,
        in_specs=(P("dp", None, None), P("dp", "sp", None, None), P("dp", "sp", None, None)),
        out_specs=P("dp", None, None),
        check_vma=False,
    )
```

time: 278 us -> 192 us (0.69)
  Pallas kernels: 0 us -> 144 us
  matrix products: 123 us -> 0 us
  waiting for transfers between devices: 83 us -> 14.3 us
  other arithmetic: 34.1 us -> 5.3 us
  local copies, waits for them, and re-layouts: 23.8 us -> 3.47 us
  blocking collectives: 0 us -> 11.3 us
    pallas_call x0 -> x1, Pallas kernels: none -> 144 us  [local_attention(): pl.pallas_call(kern, out_shape=[jax.ShapeDtypeStruct((seqs, heads, head),...]
    dot_general x2 -> x0, matrix products: 123 us -> none  [einsum(): return jnp.einsum(form, a.astype(jnp.float32), b.astype(jnp.float32))]
    all_gather x1, waiting for transfers between devices: 82.9 us -> 14.3 us  [step(): o = lax.all_gather(o, 'sp').astype(jnp.float32)]
    reduce_sum x3 -> x2, other arithmetic: 18.9 us -> 3.92 us  [the longest x1 3.9 us: step(): jnp.sum(o * w[..., None], 0) / jnp.sum(l * w, 0)[..., None]]
    unnamed x4 -> x0, local copies, waits for them, and re-layouts: 12 us -> none
    slice x1 -> x0, other arithmetic: 11.6 us -> none  [together(): seen, total, high = (parts[..., :-2], parts[..., -2:-1], parts[..., -1:])]
    all_gather x0 -> x1, blocking collectives: none -> 11.3 us  [step(): st = lax.all_gather(jnp.stack([l, m]), 'sp')]
    broadcast_in_dim x2 -> x0, local copies, waits for them, and re-layouts: 4.67 us -> none  [the longest x1 3.01 us: part_of(): high = jnp.max(scores, -1, keepdims=True)]
  transfers between devices with their start and end apart: 1 -> 1, of which waited for: 1 -> 1; matrix products, arithmetic and copies ran while one was open for 0% -> 2% of each run, Pallas kernels for 0% -> 0%
where the time goes in v1:
time: 192 us
  Pallas kernels  144 us (75%)
  waiting for transfers between devices  14.3 us (7%)
  between operations  13.4 us (7%)
  blocking collectives  11.3 us (6%)
  other arithmetic  5.3 us (3%)
  local copies, waits for them, and re-layouts  3.47 us (2%)
    pallas_call x1, Pallas kernels, local_attention(): pl.pallas_call(kern, out_shape=[jax.ShapeDtypeStruct((seqs, heads, head),...  144 us
    all_gather x1, waiting for transfers between devices, step(): o = lax.all_gather(o, 'sp').astype(jnp.float32)  14.3 us
    all_gather x1, blocking collectives, step(): st = lax.all_gather(jnp.stack([l, m]), 'sp')  11.3 us
    reduce_sum x1, other arithmetic, step(): jnp.sum(o * w[..., None], 0) / jnp.sum(l * w, 0)[..., None]  3.9 us
  transfers between devices with their start and end apart: 1, of which 1 were waited for; matrix products, arithmetic and copies ran while one was open for 2% of the time, Pallas kernels for 0%

profile of v1, /device:TPU:0, one launch (start us, length us, event | category | flops | bytes accessed | tf_op | source)
XLA Modules:
  0.0 192.0 jit_solution(10092789342076746600)
XLA Ops:
  6.5 0.0 all-gather.4.cloned.1.call-start
  6.5 144.2 %shard_map.37 = (bf16[32,96,128]{2,1,0:T(8,128)(2,1)}, f32[32,96,128]{2,1,0:T(8,128)}) custom-call(bf16[32,96,128]{2,1,0:T(8,128)(2,1)} %q_ref.1, bf16[32,2048,4,2,128]{4,3,2,1,0:T(2,128)(2,1)} %bitcast.k_hbm, bf16[32,2048,4,2,128]{4,3,2,1,0:T(2,128)(2,1)} %bitcast.1.v_hbm), custom_call_target="tpu_custom_call" | custom-call | tf_op jit(solution)/shard_map/pallas_call | solution.py:80
  150.7 0.0 all-gather.4.cloned.1.call-update
  150.7 3.5 %slice_reduce_fusion.1 = (f32[32,96]{1,0:T(8,128)S(1)}, f32[32,96]{1,0:T(8,128)S(1)}) fusion(f32[32,96,128]{2,1,0:T(8,128)} %get-tuple-element.8), kind=kLoop, calls=%fused_computation.4 | loop fusion | bytes 49152 | tf_op jit(solution)/shard_map/slice | solution.py:87
  154.2 11.3 %all-gather.1 = f32[8,32,96]{2,1,0:T(8,128)S(1)} all-gather(f32[2,32,96]{2,1,0:T(8,128)S(1)} %pad_maximum_fusion), channel_id=3, replica_groups=mesh['dp'=2,'sp'=4] {'sp'}, dimensions={0}, use_global_device_ids=true | all-gather | bytes 122880 | tf_op jit(solution)/shard_map/all_gather | solution.py:94
  165.6 14.3 %all-gather.4.cloned.1.call-done = bf16[128,96,128]{2,1,0:T(8,128)(2,1)} async-done(((bf16[32,96,128]{2,1,0:T(8,128)(2,1)}), bf16[128,96,128]{2,1,0:T(8,128)(2,1)}) %all-gather.4.cloned.1.call-update) | async-done | bytes 3145744 | tf_op jit(solution)/shard_map/all_gather | solution.py:93
  179.9 3.9 %fusion = f32[32,96,128]{2,1,0:T(8,128)S(1)} fusion(bf16[4,32,96,128]{3,2,1,0:T(8,128)(2,1)} %bitcast.23, f32[4,32,96]{2,1,0:T(8,128)S(1)} %get-tuple-element.12), kind=kLoop, calls=%fused_computation.1 | loop fusion | flops 4325376 | bytes 4767744 | tf_op jit(solution)/shard_map/reduce_sum | solution.py:97
  183.8 1.4 divide_convert_fusion
  (3 shorter events, 0.0 us)
Async XLA Ops:
  6.5 173.3 %all-gather.4.cloned.1.call-start = ((), (), s32[]{:S(2)}) async-start(), calls=%async_computation | async-start | bytes 3932160 | tf_op jit(solution)/shard_map/all_gather | solution.py:93
Sparse Core Ops, SparseCore 0:
  150.9 28.9 all-gather.3

commit v2 on v0

v2 whole, which is shorter than its diff:
```python
import jax
import jax.numpy as jnp
from jax import lax
from jax.experimental import pallas as pl
from jax.experimental.pallas import tpu as pltpu
from jax.sharding import PartitionSpec as P

AXIS = "sp"
NBUF = 3
LAG = 3
TILE = 16
CHUNK = 256


def attention(q, k, v, devices):
    seqs, heads, head = q.shape
    length, kv_heads = k.shape[1:3]
    share = heads // kv_heads
    half = heads // 2
    pairs = kv_heads // 2
    rows = 2 * length
    runs = TILE // 2
    run = length // runs
    scale = head**-0.5 * 1.4426950408889634
    k = k.reshape(seqs, length, pairs, 2, head)
    v = v.reshape(seqs, length, pairs, 2, head)

    def kern(q_hbm, k_hbm, v_hbm, o_hbm, qb, kb, vb, sb, part, stat, ob, sem, qo_sem, send_sem, recv_sem):
        me = lax.axis_index(AXIS)
        peers = [lax.rem(me + d, devices) for d in range(1, devices)]

        def fetch(b, slot):
            for a, (src, dst) in enumerate(((k_hbm, kb), (v_hbm, vb))):
                for i in range(pairs):
                    for u in range(runs):
                        pltpu.make_async_copy(src.at[b, pl.ds(u * run, run), i], dst.at[slot, i, :, pl.ds(2 * u, 2), :], sem.at[slot, a]).start()

        def fetched(slot, a):
            dst = (kb, vb)[a].at[slot]
            pltpu.make_async_copy(dst, dst, sem.at[slot, a]).wait()

        def both(ref, slot, j, lo):
            return jnp.concatenate([ref.at[slot, 2 * j + i].reshape(rows, head)[pl.ds(lo, CHUNK), :] for i in range(2)], 1)

        def sends(b):
            out = []
            for d, peer in enumerate(peers):
                for a, ref in enumerate((part, stat)):
                    own = ref.at[me, b]
                    out.append(pltpu.make_async_remote_copy(own, own, send_sem.at[d, a], recv_sem.at[b, me, a], device_id={AXIS: peer}))
            return out

        def together(b):
            for d, peer in enumerate(peers):
                for a, ref in enumerate((part, stat)):
                    theirs = ref.at[peer, b]
                    pltpu.make_async_remote_copy(theirs, theirs, send_sem.at[d, a], recv_sem.at[b, peer, a], device_id={AXIS: peer}).wait_recv()
            stats = [stat[p, b] for p in range(devices)]
            high = stats[0][0:1]
            for s in stats[1:]:
                high = jnp.maximum(high, s[0:1])
            w = [jnp.exp2((s[0:1] - high) * scale) for s in stats]
            total = w[0] * stats[0][1:2]
            for p in range(1, devices):
                total = total + w[p] * stats[p][1:2]
            sub = lax.broadcasted_iota(jnp.int32, (8, head), 0)
            table = jnp.zeros((8, head), jnp.float32)
            for p in range(devices):
                table = jnp.where(sub == p, w[p] / total, table)
            table = table.T
            out = part[0, b].astype(jnp.float32) * table[:heads, 0:1]
            for p in range(1, devices):
                out = out + part[p, b].astype(jnp.float32) * table[:heads, p : p + 1]
            ob[b] = out.astype(jnp.bfloat16)
            pltpu.make_async_copy(ob.at[b], o_hbm.at[b], qo_sem.at[1]).start()

        barrier = pltpu.get_barrier_semaphore()
        for peer in peers:
            pl.semaphore_signal(barrier, inc=1, device_id={AXIS: peer})
        fetch_q = pltpu.make_async_copy(q_hbm, qb, qo_sem.at[0])
        fetch_q.start()
        for s in range(NBUF - 1):
            fetch(s, s)
        fetch_q.wait()
        pl.semaphore_wait(barrier, devices - 1)

        row = lax.broadcasted_iota(jnp.int32, (half, CHUNK), 0)
        lane = lax.broadcasted_iota(jnp.int32, (half, CHUNK), 1)
        valid = lax.rem(lax.div(row, share), 2) == lax.rem(lane, 2)
        first = row[:, :head] < half // 2

        @pl.loop(0, seqs)
        def _(b):
            slot = lax.rem(b, NBUF)

            @pl.when(b + NBUF - 1 < seqs)
            def _():
                fetch(b + NBUF - 1, lax.rem(b + NBUF - 1, NBUF))

            @pl.when(b >= LAG)
            def _():
                together(b - LAG)

            fetched(slot, 0)
            highs = []
            for j in range(2):
                qj = qb[b, pl.ds(half * j, half), :]
                zero = jnp.zeros_like(qj)
                q2 = jnp.concatenate([jnp.where(first, qj, zero), jnp.where(first, zero, qj)], 1)
                mx = jnp.full((half, head), -jnp.inf, jnp.float32)
                for n in range(rows // CHUNK):
                    s = lax.dot_general(q2, both(kb, slot, j, n * CHUNK), (((1,), (1,)), ((), ())), preferred_element_type=jnp.float32)
                    s = jnp.where(valid, s, -jnp.inf)
                    sb[j, :, pl.ds(n * CHUNK, CHUNK)] = s
                    mx = jnp.maximum(mx, jnp.maximum(s[:, :head], s[:, head:]))
                highs.append(jnp.max(mx, 1, keepdims=True))
            fetched(slot, 1)
            high_row = jnp.zeros((1, head), jnp.float32)
            total_row = jnp.zeros((1, head), jnp.float32)
            for j in range(2):
                total = jnp.zeros((half, head), jnp.float32)
                seen = jnp.zeros((half, 2 * head), jnp.float32)
                for n in range(rows // CHUNK):
                    w = jnp.exp2((sb[j, :, pl.ds(n * CHUNK, CHUNK)] - highs[j]) * scale)
                    total = total + w[:, :head] + w[:, head:]
                    seen = seen + jnp.dot(w.astype(jnp.bfloat16), both(vb, slot, j, n * CHUNK), preferred_element_type=jnp.float32)
                part[me, b, pl.ds(half * j, half), :] = jnp.where(first, seen[:, :head], seen[:, head:]).astype(jnp.bfloat16)
                own = row[:, :head] + half * j == lane[:, :head]
                high_row = high_row + jnp.sum(jnp.where(own, highs[j], 0.0), 0, keepdims=True)
                total_row = total_row + jnp.sum(jnp.where(own, jnp.sum(total, 1, keepdims=True), 0.0), 0, keepdims=True)
            sub = lax.broadcasted_iota(jnp.int32, (8, head), 0)
            stat[me, b] = jnp.where(sub == 0, high_row, jnp.where(sub == 1, total_row, 0.0))

            @pl.when(b > 0)
            def _():
                for c in sends(b - 1):
                    c.wait_send()

            for c in sends(b):
                c.start()

        @pl.loop(seqs - LAG, seqs)
        def _(b):
            together(b)

        for c in sends(seqs - 1):
            c.wait_send()
        pltpu.make_async_copy(ob, o_hbm, qo_sem.at[1]).wait()

    buf = pltpu.VMEM((NBUF, pairs, rows // TILE, TILE, head), jnp.bfloat16)
    return pl.pallas_call(
        kern,
        out_shape=jax.ShapeDtypeStruct(q.shape, q.dtype),
        in_specs=[pl.BlockSpec(memory_space=pl.ANY)] * 3,
        out_specs=pl.BlockSpec(memory_space=pl.ANY),
        scratch_shapes=[
            pltpu.VMEM(q.shape, q.dtype),
            buf,
            buf,
            pltpu.VMEM((2, half, rows), jnp.float32),
            pltpu.VMEM((devices, seqs, heads, head), jnp.bfloat16),
            pltpu.VMEM((devices, seqs, 8, head), jnp.float32),
            pltpu.VMEM(q.shape, q.dtype),
            pltpu.SemaphoreType.DMA((NBUF, 2)),
            pltpu.SemaphoreType.DMA((2,)),
            pltpu.SemaphoreType.DMA((devices - 1, 2)),
            pltpu.SemaphoreType.DMA((seqs, devices, 2)),
        ],
        compiler_params=pltpu.CompilerParams(vmem_limit_bytes=60 << 20, collective_id=0, has_side_effects=True),
        cost_estimate=pl.CostEstimate(flops=4 * heads * head * length * seqs, bytes_accessed=2 * k.size * 2, transcendentals=heads * length * seqs),
    )(q, k, v)


def solution(mesh):
    return jax.shard_map(
        lambda q, k, v: attention(q, k, v, mesh.shape[AXIS]),
        mesh=mesh,
        in_specs=(P("dp", None, None), P("dp", AXIS, None, None), P("dp", AXIS, None, None)),
        out_specs=P("dp", None, None),
        check_vma=False,
    )
```

time: 278 us -> 102 us (0.37)
  matrix products: 123 us -> 0 us
  Pallas kernels: 0 us -> 100 us
  waiting for transfers between devices: 83 us -> 0 us
  other arithmetic: 34.1 us -> 0 us
  local copies, waits for them, and re-layouts: 23.8 us -> 2.06 us
  between operations: 13.5 us -> 0.01 us
    dot_general x2 -> x0, matrix products: 123 us -> none  [einsum(): return jnp.einsum(form, a.astype(jnp.float32), b.astype(jnp.float32))]
    pallas_call x0 -> x1, Pallas kernels: none -> 100 us  [attention(): pl.pallas_call(kern, out_shape=jax.ShapeDtypeStruct(q.shape, q.dtype), in...]
    all_gather x1 -> x0, waiting for transfers between devices: 82.9 us -> none  [step(): return together(lax.all_gather(part_of(q, k, v), 'sp')).reshape(q.shape)]
    reduce_sum x3 -> x0, other arithmetic: 18.9 us -> none  [the longest x1 14.2 us: part_of(): jnp.sum(weights, -1, keepdims=True)]
    slice x1 -> x0, other arithmetic: 11.6 us -> none  [together(): seen, total, high = (parts[..., :-2], parts[..., -2:-1], parts[..., -1:])]
    unnamed x4 -> x1, local copies, waits for them, and re-layouts: 12 us -> 2.06 us
    broadcast_in_dim x2 -> x0, local copies, waits for them, and re-layouts: 4.67 us -> none  [the longest x1 3.01 us: part_of(): high = jnp.max(scores, -1, keepdims=True)]
    concatenate x1 -> x0, local copies, waits for them, and re-layouts: 4.52 us -> none  [part_of(): jnp.concatenate([seen, jnp.sum(weights, -1, keepdims=True), high], -1)]
  transfers between devices with their start and end apart: 1 -> 0, of which waited for: 1 -> 0; matrix products, arithmetic and copies ran while one was open for 0% -> 0% of each run, Pallas kernels for 0% -> 0%
where the time goes in v2:
time: 102 us
  Pallas kernels  100 us (98%)
  local copies, waits for them, and re-layouts  2.06 us (2%)
    pallas_call x1, Pallas kernels, attention(): pl.pallas_call(kern, out_shape=jax.ShapeDtypeStruct(q.shape, q.dtype), in...  100 us
    unnamed x1, local copies, waits for them, and re-layouts  2.06 us

profile of v2, /device:TPU:0, one launch (start us, length us, event | category | flops | bytes accessed | tf_op | source)
XLA Modules:
  0.0 102.3 jit_solution(12937173617342954300)
XLA Ops:
  0.0 100.2 %shard_map.37 = bf16[32,96,128]{2,1,0:T(8,128)(2,1)} custom-call(bf16[32,96,128]{2,1,0:T(8,128)(2,1)} %q_hbm.1, bf16[32,2048,4,2,128]{4,3,2,1,0:T(2,128)(2,1)} %bitcast.k_hbm, bf16[32,2048,4,2,128]{4,3,2,1,0:T(2,128)(2,1)} %bitcast.1.v_hbm), custom_call_target="tpu_custom_call" | custom-call | flops 3221225472 | bytes 268435456 | tf_op jit(solution)/shard_map/pallas_call | solution.py:151
  100.2 2.1 %copy.5 = bf16[32,96,128]{2,1,0:T(8,128)(2,1)} copy(bf16[32,96,128]{2,1,0:T(8,128)(2,1)} %shard_map.37) | data formatting | bytes 1572864
